TPU v7x, 32 devices: a whole 2x2x4 slice. The times are simulated.
32 devices in a mesh: samp: 8 (over z, y), gene: 4 (over x, core).
Axes of the slice: x: 2, y: 2, z: 4, core: 2. Of those that a mesh axis runs over, the one named last changes fastest.
Arguments:
- genotypes: int32 [256, 4096], P('samp', 'gene'), may hold values from -2147483648 to 1789569706, as said below
- allele_freq: float32 [4096], P('gene'), may hold values from 0.035 to 0.56
- sample_weight: float32 [16, 256], P(None, 'samp'), may hold values from 0.2 to 2
- residual: float32 [16, 256], P(None, 'samp'), may hold values from -12 to 12
- variant_weight: float32 [4096], P('gene'), may hold values from 0.2 to 4
- block_gene: int32 [32], replicated, may hold values from 0 to 15, as said below
- gene_variants: int32 [16], replicated, may hold values from 1 to 384, as said below
Outputs:
- burden_z: float32 [16], replicated
- skat_z: float32 [16], replicated
Inputs may be any that keep to these rules, and one draw needn't show every extreme that they name: Each word holds 16 dosages 0, 1 or 2: bits 2k and 2k+1 of genotypes[i, v] are the dosage of variant slot v in sample (k, i); a dosage 2 in the top field sets the sign bit. `block_gene`: never falling; the blocks come in aligned groups of four, each shared by two consecutive genes, so every gene has 1 to 3 blocks. `gene_variants`: A gene with m blocks has from (m - 1) * 128 + 1 to m * 128 live variants; the slots after them in its last block are padding.
All inputs are finite; a program needn't handle non-finite values.
Results may differ from a plain program's by a relative error of at most 0.0037.
Values sent between devices are 32-bit elements; how exact they have to be, the bound alone decides.
A program may use at most 64 MiB of HBM per device.

v0:
```python
import jax
import jax.numpy as jnp
from jax import lax
from jax.sharding import PartitionSpec as P

BLK = 128


def unpack(packed_words, allele_part, root_weight):
    fields = root_weight.shape[0]
    offsets = 2 * jnp.arange(fields, dtype=jnp.int32)
    dosage = jnp.bitwise_and(jnp.right_shift(packed_words[None, :, :], offsets[:, None, None]), 3)
    centered = dosage.astype(jnp.float32) - 2.0 * allele_part[None, None, :]
    return (root_weight[:, :, None] * centered).astype(jnp.bfloat16)


def block_grams(scaled, block_count):
    stacked = scaled.reshape(scaled.shape[0] * scaled.shape[1], block_count, BLK)
    return jnp.einsum("sbu,sbv->buv", stacked, stacked, preferred_element_type=jnp.float32)


def block_stats(gram_part, scores, effective):
    weighted_score = effective * scores
    burden_sum = jnp.sum(weighted_score, axis=1)
    skat_sum = jnp.sum(weighted_score * weighted_score, axis=1)
    image = jnp.einsum("buv,bv->bu", gram_part, effective, precision=lax.Precision.HIGHEST)
    burden_var = jnp.sum(effective * image, axis=1)
    diagonal = jnp.diagonal(gram_part, axis1=1, axis2=2)
    trace_one = jnp.sum(effective * effective * diagonal, axis=1)
    scaled_gram = effective[:, :, None] * gram_part * effective[:, None, :]
    trace_two = jnp.sum(scaled_gram * scaled_gram, axis=(1, 2))
    return jnp.stack([burden_sum, burden_var, skat_sum, trace_one, trace_two])


def live_weights(block_ids, variant_part, block_gene, gene_variants):
    total_blocks = block_gene.shape[0]
    genes = gene_variants.shape[0]
    chosen = block_ids[:, None] == jnp.arange(total_blocks, dtype=jnp.int32)[None, :]
    gene_of = jnp.sum(jnp.where(chosen, block_gene[None, :], 0), axis=1)
    first_block = jnp.sum((block_gene[None, :] < gene_of[:, None]).astype(jnp.int32), axis=1)
    member = gene_of[:, None] == jnp.arange(genes, dtype=jnp.int32)[None, :]
    counted = jnp.sum(jnp.where(member, gene_variants[None, :], 0), axis=1)
    column = jnp.arange(BLK, dtype=jnp.int32)
    is_live = (block_ids - first_block)[:, None] * BLK + column[None, :] < counted[:, None]
    return (variant_part * is_live.astype(jnp.float32), member.astype(jnp.float32))


def local(
    genotypes, allele_freq, sample_weight, residual, variant_weight, block_gene, gene_variants
):
    local_blocks = genotypes.shape[1] // BLK
    owned_count = local_blocks // lax.axis_size("samp")
    samp_index = lax.axis_index("samp")
    gene_index = lax.axis_index("gene")
    block_ids = (
        gene_index * local_blocks
        + samp_index * owned_count
        + jnp.arange(owned_count, dtype=jnp.int32)
    )
    variant_blocks = variant_weight.reshape(local_blocks, BLK)
    own_weights = lax.dynamic_slice_in_dim(variant_blocks, samp_index * owned_count, owned_count, 0)
    effective, member = live_weights(block_ids, own_weights, block_gene, gene_variants)
    own_words = lax.all_to_all(genotypes, "samp", split_axis=1, concat_axis=0, tiled=True)
    all_weight, all_residual = (
        lax.all_gather(sample_weight, "samp", axis=1, tiled=True),
        lax.all_gather(residual, "samp", axis=1, tiled=True),
    )
    own_freq = lax.dynamic_slice_in_dim(
        allele_freq, samp_index * owned_count * BLK, owned_count * BLK, 0
    )
    root_all = jnp.sqrt(all_weight)
    weighted_residual = (root_all * all_residual).astype(jnp.bfloat16)
    scaled = unpack(own_words, own_freq, root_all)
    gram_part = block_grams(scaled, owned_count)
    flattened = scaled.reshape(scaled.shape[0] * scaled.shape[1], owned_count * BLK)
    scores = jnp.dot(
        weighted_residual.reshape(1, -1), flattened, preferred_element_type=jnp.float32
    )
    variance = jnp.sum(all_weight * all_residual * all_residual) / (
        all_weight.shape[0] * all_weight.shape[1]
    )
    gene_parts = jnp.dot(
        block_stats(gram_part, scores, effective), member, precision=lax.Precision.HIGHEST
    )
    totals = lax.psum(gene_parts, ("samp", "gene"))
    burden = totals[0] / jnp.sqrt(variance * totals[1])
    skat_score = (totals[2] - variance * totals[3]) / (variance * jnp.sqrt(2.0 * totals[4]))
    return (burden, skat_score)


def solution(mesh):
    placed = (P("samp", "gene"), P("gene"), P(None, "samp"), P(None, "samp"), P("gene"), P(), P())
    return jax.shard_map(local, mesh=mesh, in_specs=placed, out_specs=(P(), P()), check_vma=False)
```

profile of v0, /device:TPU:0, one launch (start us, length us, event | category | flops | bytes accessed | tf_op | source)
XLA Modules:
  0.0 128.4 jit_solution(14625321429608748185)
XLA Ops:
  0.6 0.0 copy-start
  0.6 0.9 copy-done
  1.5 0.6 copy_bitcast_fusion
  2.2 0.0 copy-start.3
  2.2 0.0 copy-start.1
  2.2 7.4 %all-to-all-start = ((s32[32,8,128]{2,0,1:T(8,128)}), s32[32,8,128]{2,0,1:T(8,128)S(1)}, u32[]{:S(2)}, u32[]{:S(2)}) async-start(s32[32,8,128]{2,0,1:T(8,128)} %copy_bitcast_fusion), calls=%async_computation | async-start | bytes 262144 | tf_op jit(solution)/shard_map/all_to_all | solution.py:63
  9.6 0.0 copy-done.3
  9.7 0.6 fusion.16
  10.3 0.6 fusion.19
  10.9 1.3 fusion.17
  12.2 0.0 copy-done.1
  12.2 0.0 copy-start.2
  12.2 31.2 %all-gather.1 = f32[8,32,16]{1,2,0:T(8,128)S(1)} all-gather(f32[1,32,16]{1,2,0:T(8,128)S(1)} %bitcast.67), channel_id=1, replica_groups=mesh['samp'=8,'gene'=4] {'samp'}, dimensions={0}, use_global_device_ids=true | all-gather | bytes 18432 | tf_op jit(solution)/shard_map/all_gather | solution.py:66
  43.4 0.1 reshape.172
  43.5 0.0 copy-done.2
  43.5 30.5 %all-gather = f32[8,32,16]{1,2,0:T(8,128)S(1)} all-gather(f32[1,32,16]{1,2,0:T(8,128)S(1)} %bitcast.68), channel_id=1, replica_groups=mesh['samp'=8,'gene'=4] {'samp'}, dimensions={0}, use_global_device_ids=true | all-gather | bytes 18432 | tf_op jit(solution)/shard_map/all_gather | solution.py:65
  74.1 0.0 copy-start.4
  74.1 0.1 reshape.170
  74.2 0.6 fusion.12
  76.0 0.8 dynamic-slice_multiply_fusion
  76.8 0.0 copy-done.4
  76.8 1.3 fusion.18
  78.1 0.0 all-to-all-done
  78.1 0.1 copy.22
  78.2 0.9 convolution_bitcast_fusion
  79.1 1.2 gather_fusion
  80.4 1.9 %fusion.20 = (f32[]{:T(128)}, f32[1,128]{1,0:T(1,128)S(1)}) fusion(f32[128]{0:T(128)S(1)} %gather_fusion, f32[8,128]{1,0:T(8,128)} %bitcast.70, s32[]{:T(128)S(6)} %select_n.22, s32[]{:T(128)} %fusion.18, s32[]{:T(128)S(6)} %mul.106), kind=kLoop, calls=%fused_computation.37 | loop fusion | flops 767 | bytes 1552 | tf_op jit(solution)/shard_map/reduce_sum | solution.py:29
  82.3 0.8 fusion.11
  83.1 1.2 multiply_reduce_fusion.1
  84.4 0.7 multiply_reduce_fusion
  85.1 3.3 %stack.23 = f32[5,1]{0,1:T(1,128)S(1)} concatenate(f32[1,1]{0,1:T(1,128)} %bitcast.12, f32[1,1]{0,1:T(1,128)} %bitcast.17, f32[1,1]{0,1:T(1,128)} %bitcast.18, f32[1,1]{0,1:T(1,128)} %bitcast.21, f32[1,1]{0,1:T(1,128)} %bitcast.22), dimensions={0} | concatenate | bytes 40 | tf_op jit(solution)/shard_map/stack | solution.py:32
  88.3 0.1 broadcast_multiply_fusion
  88.4 39.5 %psum.7 = f32[5,16]{1,0:T(8,128)S(1)} all-reduce(f32[5,16]{1,0:T(8,128)S(1)} %broadcast_multiply_fusion), channel_id=1, replica_groups=mesh['samp'=8,'gene'=4] {'samp','gene'}, use_global_device_ids=true, to_apply=%region_8.9 | all-reduce | flops 80 | bytes 640 | tf_op jit(solution)/shard_map/psum | solution.py:85
  127.9 0.5 fusion.22
  (4 shorter events, 0.1 us)
Async XLA Ops:
  0.6 0.9 copy-start
  2.2 7.5 %copy-start.3 = (s32[32]{0:T(128)S(1)}, s32[32]{0:T(128)}, u32[]{:S(2)}) copy-start(s32[32]{0:T(128)} %param.12) | copy-start | bytes 388
  2.2 10.0 %copy-start.1 = (f32[16,32]{1,0:T(8,128)S(1)}, f32[16,32]{1,0:T(8,128)}, u32[]{:S(2)}) copy-start(f32[16,32]{1,0:T(8,128)} %param.10) | copy-start | bytes 6148
  2.2 75.9 %all-to-all-start = ((s32[32,8,128]{2,0,1:T(8,128)}), s32[32,8,128]{2,0,1:T(8,128)S(1)}, u32[]{:S(2)}, u32[]{:S(2)}) async-start(s32[32,8,128]{2,0,1:T(8,128)} %copy_bitcast_fusion), calls=%async_computation | async-start | bytes 262144 | tf_op jit(solution)/shard_map/all_to_all | solution.py:63
  12.2 31.3 %copy-start.2 = (f32[16,32]{1,0:T(8,128)S(1)}, f32[16,32]{1,0:T(8,128)}, u32[]{:S(2)}) copy-start(f32[16,32]{1,0:T(8,128)} %param.9) | copy-start | bytes 6148
  74.1 2.7 %copy-start.4 = (s32[16]{0:T(128)S(1)}, s32[16]{0:T(128)}, u32[]{:S(2)}) copy-start(s32[16]{0:T(128)} %param.13) | copy-start | bytes 196
where the time goes:
time: 129 us; the launch traced here: 128 us
  blocking collectives  101 us (78%)
  other arithmetic  8.47 us (7%)
  starting transfers between devices  7.44 us (6%)
  local copies, waits for them, and re-layouts  6.39 us (5%)
  matrix products  2.98 us (2%)
  between operations  1.93 us (1%)
    psum x1, blocking collectives, local(): totals = lax.psum(gene_parts, ('samp', 'gene'))  39.5 us
    all_gather x1, blocking collectives, local(): lax.all_gather(residual, 'samp', axis=1, tiled=True)  31.2 us
    all_gather x1, blocking collectives, local(): lax.all_gather(sample_weight, 'samp', axis=1, tiled=True)  30.5 us
    all_to_all x1, starting transfers between devices, local(): lax.all_to_all(genotypes, 'samp', split_axis=1, concat_axis=0, tiled=True)  7.44 us
    another operation x1, local copies, waits for them, and re-layouts, block_stats(): return jnp.stack([burden_sum, burden_var, skat_sum, trace_one, trace_two])  3.27 us
  transfers between devices with their start and end apart: 1, of which 0 were waited for; matrix products, arithmetic and copies ran while one was open for 4% of the time, Pallas kernels for 0%

commit v1 on v0

v1 whole, which is shorter than its diff:
```python
import functools

import jax
import jax.numpy as jnp
from jax import lax
from jax.experimental import pallas as pl
from jax.experimental.pallas import tpu as pltpu
from jax.sharding import PartitionSpec as P

BLK = 128
MESH = pl.DeviceIdType.MESH
STATS = 5


def lane_sum(row):
    return jnp.sum(row, axis=1, keepdims=True)


def kernel(
    samp_size,
    gene_size,
    genotypes_hbm,
    freq_hbm,
    weight_hbm,
    residual_hbm,
    variant_hbm,
    block_gene_hbm,
    counts_hbm,
    burden_ref,
    skat_ref,
    words_in,
    freq_in,
    weight_in,
    residual_in,
    variant_in,
    block_gene_in,
    counts_in,
    tile_out,
    tiles,
    words,
    scaled,
    root_rows,
    residual_rows,
    pair_weight,
    row_out,
    rows,
    load_sem,
    send_sem,
    tile_sem,
    word_sem,
    row_send_sem,
    row_sem,
):
    devices = samp_size * gene_size
    samp = lax.axis_index("samp")
    gene = lax.axis_index("gene")
    me = samp * gene_size + gene
    fields, local_rows = weight_in.shape
    half = fields // 2
    group = BLK // local_rows
    chunks = samp_size // group
    owned = words.shape[1] // BLK
    local_blocks = freq_in.shape[0]
    genes = counts_in.shape[1]
    width = row_out.shape[1]

    def device_of(index):
        return {"samp": lax.div(index, gene_size), "gene": lax.rem(index, gene_size)}

    barrier = pltpu.get_barrier_semaphore()

    @pl.loop(1, devices)
    def _(step):
        pl.semaphore_signal(
            barrier,
            inc=1,
            device_id=device_of(lax.rem(me + step, devices)),
            device_id_type=MESH,
        )

    loads = [
        pltpu.make_async_copy(source, target, load_sem.at[place])
        for place, (source, target) in enumerate(
            (
                (weight_hbm, weight_in),
                (residual_hbm, residual_in),
                (genotypes_hbm, words_in),
                (freq_hbm, freq_in),
                (variant_hbm, variant_in),
                (block_gene_hbm, block_gene_in),
                (counts_hbm, counts_in),
            )
        )
    ]
    for load in loads:
        load.start()
    loads[0].wait()
    loads[1].wait()
    own_weight, own_residual = weight_in[...], residual_in[...]
    own_tile = jnp.concatenate(
        [own_weight[:half], own_weight[half:], own_residual[:half], own_residual[half:]], axis=1
    )
    tile_out[...] = own_tile
    tiles[samp] = own_tile
    for load in loads[2:]:
        load.wait()
    pl.semaphore_wait(barrier, devices - 1)

    def tile_copy(peer, slot):
        return pltpu.make_async_remote_copy(
            src_ref=tile_out,
            dst_ref=tiles.at[samp],
            send_sem=send_sem.at[0],
            recv_sem=tile_sem.at[slot],
            device_id={"samp": peer, "gene": gene},
            device_id_type=MESH,
        )

    def word_copy(peer, slot):
        start = pl.multiple_of(peer * (owned * BLK), BLK)
        return pltpu.make_async_remote_copy(
            src_ref=words_in.at[:, pl.ds(start, owned * BLK)],
            dst_ref=words.at[pl.ds(pl.multiple_of(samp * local_rows, local_rows), local_rows), :],
            send_sem=send_sem.at[1],
            recv_sem=word_sem.at[slot],
            device_id={"samp": peer, "gene": gene},
            device_id_type=MESH,
        )

    @pl.loop(1, samp_size)
    def _(step):
        tile_copy(lax.rem(samp + step, samp_size), samp).start()

    @pl.loop(1, samp_size)
    def _(step):
        word_copy(lax.rem(samp + step, samp_size), samp).start()

    own_start = pl.multiple_of(samp * (owned * BLK), BLK)
    own_place = pl.multiple_of(samp * local_rows, local_rows)
    words[pl.ds(own_place, local_rows), :] = words_in[:, pl.ds(own_start, owned * BLK)]

    block_gene = block_gene_in[...].astype(jnp.float32)
    counts = counts_in[...].astype(jnp.float32)
    block_lane = lax.broadcasted_iota(jnp.int32, block_gene.shape, 1)
    gene_lane = lax.broadcasted_iota(jnp.int32, counts.shape, 1).astype(jnp.float32)
    column = lax.broadcasted_iota(jnp.int32, (1, BLK), 1).astype(jnp.float32)
    stat_sub = lax.broadcasted_iota(jnp.int32, (8, width), 0)
    stat_lane = lax.broadcasted_iota(jnp.int32, (8, width), 1) - stat_sub * genes
    effective, places = [], []
    for block in range(owned):
        local_block = samp * owned + block
        block_id = gene * local_blocks + local_block
        gene_of = lane_sum(jnp.where(block_lane == block_id, block_gene, 0.0))
        first = lane_sum(jnp.where(block_gene < gene_of, 1.0, 0.0))
        counted = lane_sum(jnp.where(gene_lane == gene_of, counts, 0.0))
        block_float = jnp.zeros((1, 1), jnp.float32) + block_id.astype(jnp.float32)
        live = (block_float - first) * BLK + column < counted
        weights = jnp.where(live, variant_in[pl.ds(local_block, 1), :], 0.0)
        effective.append(weights)
        across = jnp.broadcast_to(weights, (BLK, BLK))
        pair_weight[block] = across * across.T
        member = stat_lane.astype(jnp.float32) == gene_of
        places.append(jnp.where(member & (stat_sub < STATS), 1.0, 0.0))

    def wait_tile(peer):
        pltpu.make_async_copy(tile_out, tiles.at[peer], tile_sem.at[peer]).wait()

    def wait_words(peer):
        place = words.at[pl.ds(pl.multiple_of(peer * local_rows, local_rows), local_rows), :]
        pltpu.make_async_copy(place, place, word_sem.at[peer]).wait()

    @pl.loop(1, samp_size)
    def _(step):
        wait_tile(lax.rem(samp + step, samp_size))

    power = jnp.zeros((half, BLK), jnp.float32)
    for chunk in range(chunks):
        parts = [tiles[chunk * group + peer] for peer in range(group)]
        kinds = [
            jnp.concatenate(
                [part[:, kind * local_rows : (kind + 1) * local_rows] for part in parts], axis=1
            )
            for kind in range(4)
        ]
        for upper in range(2):
            weight, resid = kinds[upper], kinds[2 + upper]
            root = jnp.sqrt(weight)
            power = power + weight * resid * resid
            root_rows[chunk, upper * half : (upper + 1) * half, :] = root
            residual_rows[chunk, upper * half : (upper + 1) * half, :] = root * resid
    variance = lane_sum(jnp.sum(power, axis=0, keepdims=True)) / (
        fields * local_rows * samp_size
    )

    @pl.loop(1, samp_size)
    def _(step):
        wait_words(lax.rem(samp + step, samp_size))

    message = jnp.zeros((8, width), jnp.float32)
    diagonal = lax.broadcasted_iota(jnp.int32, (BLK, BLK), 0) == lax.broadcasted_iota(
        jnp.int32, (BLK, BLK), 1
    )
    for block in range(owned):
        twice = 2.0 * jnp.broadcast_to(
            freq_in[pl.ds(samp * owned + block, 1), :], (BLK, BLK)
        ).T

        def chunk_gram(chunk, total, block=block, twice=twice):
            start = pl.multiple_of(chunk * BLK, BLK)
            turned = words[pl.ds(start, BLK), block * BLK : (block + 1) * BLK].T
            for field in range(fields):
                dosage = jnp.bitwise_and(jnp.right_shift(turned, 2 * field), 3)
                root = root_rows[chunk, field : field + 1, :]
                value = (root * (dosage.astype(jnp.float32) - twice)).astype(jnp.bfloat16)
                score = residual_rows[chunk, field : field + 1, :]
                lanes = slice(field * BLK, (field + 1) * BLK)
                scaled[:BLK, lanes] = value
                scaled[BLK:, lanes] = jnp.broadcast_to(score, (16, BLK)).astype(jnp.bfloat16)
            return total + lax.dot_general(
                scaled[...],
                scaled[:BLK, :],
                (((1,), (1,)), ((), ())),
                preferred_element_type=jnp.float32,
            )

        total = jnp.zeros((BLK + 16, BLK), jnp.float32)
        if chunks <= 2:
            for chunk in range(chunks):
                total = chunk_gram(chunk, total)
        else:
            total = lax.fori_loop(0, chunks, chunk_gram, total)
        weighted = total[:BLK] * pair_weight[block]
        score = effective[block] * total[BLK : BLK + 1]
        sums = [
            score,
            jnp.sum(weighted, axis=0, keepdims=True),
            score * score,
            jnp.sum(jnp.where(diagonal, weighted, 0.0), axis=0, keepdims=True),
            jnp.sum(weighted * weighted, axis=0, keepdims=True),
            jnp.zeros((8 - STATS, BLK), jnp.float32),
        ]
        message = message + lane_sum(jnp.concatenate(sums, axis=0)) * places[block]
    row = jnp.sum(message, axis=0, keepdims=True)
    row_out[...] = row
    rows[me] = row

    def row_copy(index):
        return pltpu.make_async_remote_copy(
            src_ref=row_out,
            dst_ref=rows.at[me],
            send_sem=row_send_sem,
            recv_sem=row_sem,
            device_id=device_of(index),
            device_id_type=MESH,
        )

    @pl.loop(1, devices)
    def _(step):
        row_copy(lax.rem(me + step, devices)).start()

    landed = rows.at[pl.ds(0, devices - 1)]
    pltpu.make_async_copy(landed, landed, row_sem).wait()
    totals = jnp.sum(rows[...], axis=0)
    parts = [totals[:, stat * genes : (stat + 1) * genes] for stat in range(STATS)]
    burden_ref[...] = parts[0] / jnp.sqrt(variance * parts[1])
    skat_ref[...] = (parts[2] - variance * parts[3]) / (
        variance * jnp.sqrt(2.0 * parts[4])
    )

    pltpu.make_async_copy(landed, landed, row_send_sem).wait()

    sent_tiles = tiles.at[pl.ds(0, samp_size - 1)]
    pltpu.make_async_copy(sent_tiles, sent_tiles, send_sem.at[0]).wait()
    sent_words = words.at[pl.ds(0, (samp_size - 1) * local_rows), :]
    pltpu.make_async_copy(sent_words, sent_words, send_sem.at[1]).wait()


def solution(mesh):
    samp_size, gene_size = mesh.shape["samp"], mesh.shape["gene"]
    devices = samp_size * gene_size

    def local(
        genotypes, allele_freq, sample_weight, residual, variant_weight, block_gene, gene_variants
    ):
        local_rows, columns = genotypes.shape
        local_blocks = columns // BLK
        owned = local_blocks // samp_size
        fields = sample_weight.shape[0]
        genes = gene_variants.shape[0]
        width = -(-STATS * genes // BLK) * BLK
        chunks = samp_size * local_rows // BLK
        burden, skat = pl.pallas_call(
            functools.partial(kernel, samp_size, gene_size),
            out_shape=[jax.ShapeDtypeStruct((1, genes), jnp.float32)] * 2,
            in_specs=[pl.BlockSpec(memory_space=pl.ANY)] * 7,
            out_specs=[pl.BlockSpec(memory_space=pltpu.VMEM)] * 2,
            scratch_shapes=[
                pltpu.VMEM((local_rows, columns), jnp.int32),
                pltpu.VMEM((local_blocks, BLK), jnp.float32),
                pltpu.VMEM((fields, local_rows), jnp.float32),
                pltpu.VMEM((fields, local_rows), jnp.float32),
                pltpu.VMEM((local_blocks, BLK), jnp.float32),
                pltpu.VMEM((1, block_gene.shape[0]), jnp.int32),
                pltpu.VMEM((1, genes), jnp.int32),
                pltpu.VMEM((fields // 2, 4 * local_rows), jnp.float32),
                pltpu.VMEM((samp_size, fields // 2, 4 * local_rows), jnp.float32),
                pltpu.VMEM((samp_size * local_rows, owned * BLK), jnp.int32),
                pltpu.VMEM((BLK + 16, fields * BLK), jnp.bfloat16),
                pltpu.VMEM((chunks, fields, BLK), jnp.float32),
                pltpu.VMEM((chunks, fields, BLK), jnp.float32),
                pltpu.VMEM((owned, BLK, BLK), jnp.float32),
                pltpu.VMEM((1, width), jnp.float32),
                pltpu.VMEM((devices, 1, width), jnp.float32),
                pltpu.SemaphoreType.DMA((7,)),
                pltpu.SemaphoreType.DMA((2,)),
                pltpu.SemaphoreType.DMA((samp_size,)),
                pltpu.SemaphoreType.DMA((samp_size,)),
                pltpu.SemaphoreType.DMA,
                pltpu.SemaphoreType.DMA,
            ],
            compiler_params=pltpu.CompilerParams(collective_id=0, has_side_effects=True),
        )(
            genotypes,
            allele_freq.reshape(local_blocks, BLK),
            sample_weight,
            residual,
            variant_weight.reshape(local_blocks, BLK),
            block_gene.reshape(1, -1),
            gene_variants.reshape(1, -1),
        )
        return burden.reshape(-1), skat.reshape(-1)

    placed = (P("samp", "gene"), P("gene"), P(None, "samp"), P(None, "samp"), P("gene"), P(), P())
    return jax.shard_map(local, mesh=mesh, in_specs=placed, out_specs=(P(), P()), check_vma=False)
```

time: 129 us -> 21.7 us (0.17)
  blocking collectives: 101 us -> 0 us
  Pallas kernels: 0 us -> 19 us
  other arithmetic: 8.47 us -> 0 us
  starting transfers between devices: 7.44 us -> 0 us
  local copies, waits for them, and re-layouts: 6.39 us -> 1.8 us
  matrix products: 2.98 us -> 0 us
    all_gather x2 -> x0, blocking collectives: 61.7 us -> none  [the longest x1 31.2 us: local(): lax.all_gather(residual, 'samp', axis=1, tiled=True)]
    psum x1 -> x0, blocking collectives: 39.5 us -> none  [local(): totals = lax.psum(gene_parts, ('samp', 'gene'))]
    pallas_call x0 -> x1, Pallas kernels: none -> 19 us  [local(): pl.pallas_call(functools.partial(kernel, samp_size, gene_size), out_shape...]
    all_to_all x1 -> x0, starting transfers between devices: 7.44 us -> none  [local(): lax.all_to_all(genotypes, 'samp', split_axis=1, concat_axis=0, tiled=True)]
    reduce_sum x6 -> x0, other arithmetic: 6.44 us -> none  [the longest x1 1.95 us: block_stats(): trace_one = jnp.sum(effective * effective * diagonal, axis=1)]
    another operation x1 -> x0, local copies, waits for them, and re-layouts: 3.27 us -> none  [block_stats(): return jnp.stack([burden_sum, burden_var, skat_sum, trace_one, trace_two])]
    dot_general x3 -> x0, matrix products: 2.98 us -> none  [the longest x1 1.24 us: local(): jnp.dot(weighted_residual.reshape(1, -1), flattened, preferred_element_ty...]
  transfers between devices with their start and end apart: 1 -> 0, of which waited for: 0 -> 0; matrix products, arithmetic and copies ran while one was open for 4% -> 0% of each run, Pallas kernels for 0% -> 0%
where the time goes in v1:
time: 21.7 us; the launch traced here: 21.5 us
  Pallas kernels  19 us (88%)
  local copies, waits for them, and re-layouts  1.8 us (8%)
  between operations  0.65 us (3%)
    pallas_call x1, Pallas kernels, local(): pl.pallas_call(functools.partial(kernel, samp_size, gene_size), out_shape...  19 us
    unnamed x6, local copies, waits for them, and re-layouts  1.8 us

profile of v1, /device:TPU:0, one launch (start us, length us, event | category | flops | bytes accessed | tf_op | source)
XLA Modules:
  0.0 21.5 jit_solution(3001750882514873755)
XLA Ops:
  0.6 19.0 %shard_map.86 = (f32[1,16]{1,0:T(1,128)}, f32[1,16]{1,0:T(1,128)}) custom-call(s32[32,1024]{1,0:T(8,128)} %genotypes_hbm.1, f32[8,128]{1,0:T(8,128)} %bitcast.6, f32[16,32]{1,0:T(8,128)} %weight_hbm.1, f32[16,32]{1,0:T(8,128)} %residual_hbm.1, f32[8,128]{1,0:T(8,128)} %bitcast.7, s32[1,32]{1,0:T(1,128)} %bitcast.8, s32[1,16]{1,0:T(1,128)} %bitcast.9), custom_call_target="tpu_custom_call" | custom-call | tf_op jit(solution)/shard_map/pallas_call | solution.py:292
  19.6 0.0 copy-start.1
  19.7 0.7 %copy-done.1 = f32[1,16]{1,0:T(1,128)S(1)} copy-done((f32[1,16]{1,0:T(1,128)S(1)}, f32[1,16]{1,0:T(1,128)}, u32[]{:S(2)}) %copy-start.1) | copy-done | bytes 88
  20.3 0.0 copy-start
  20.3 0.5 %copy.11 = f32[16]{0:T(128)} copy(f32[16]{0:T(128)S(1)} %bitcast.11) | data formatting | bytes 128
  20.8 0.1 copy-done
  20.9 0.5 %copy.12 = f32[16]{0:T(128)} copy(f32[16]{0:T(128)S(1)} %bitcast.10) | data formatting | bytes 128
Async XLA Ops:
  19.6 0.7 %copy-start.1 = (f32[1,16]{1,0:T(1,128)S(1)}, f32[1,16]{1,0:T(1,128)}, u32[]{:S(2)}) copy-start(f32[1,16]{1,0:T(1,128)} %get-tuple-element.4) | copy-start | bytes 196
  20.3 0.6 %copy-start = (f32[1,16]{1,0:T(1,128)S(1)}, f32[1,16]{1,0:T(1,128)}, u32[]{:S(2)}) copy-start(f32[1,16]{1,0:T(1,128)} %get-tuple-element.5) | copy-start | bytes 196

commit v2 on v1

v2 whole, which is shorter than its diff:
```python
import functools

import jax
import jax.numpy as jnp
from jax import lax
from jax.experimental import pallas as pl
from jax.experimental.pallas import tpu as pltpu
from jax.sharding import PartitionSpec as P

BLK = 128
MESH = pl.DeviceIdType.MESH
STATS = 5


def lane_sum(row):
    return jnp.sum(row, axis=1, keepdims=True)


def kernel(
    samp_size,
    gene_size,
    genotypes_hbm,
    freq_hbm,
    weight_hbm,
    residual_hbm,
    variant_hbm,
    block_gene_hbm,
    counts_hbm,
    both_ref,
    words_in,
    freq_in,
    weight_in,
    residual_in,
    variant_in,
    block_gene_in,
    counts_in,
    tile_out,
    tiles,
    words,
    scaled,
    root_rows,
    residual_rows,
    power_rows,
    pair_weight,
    row_out,
    rows,
    load_sem,
    send_sem,
    tile_sem,
    word_sem,
    row_send_sem,
    row_sem,
    ready_sem,
    others_sem,
):
    devices = samp_size * gene_size
    samp = lax.axis_index("samp")
    gene = lax.axis_index("gene")
    me = samp * gene_size + gene
    fields, local_rows = weight_in.shape
    half = fields // 2
    group = BLK // local_rows
    chunks = samp_size // group
    owned = words.shape[1] // BLK
    local_blocks = freq_in.shape[0]
    genes = counts_in.shape[1]
    width = row_out.shape[1]

    loads = [
        pltpu.make_async_copy(source, target, load_sem.at[place])
        for place, (source, target) in enumerate(
            (
                (genotypes_hbm, words_in),
                (weight_hbm, weight_in),
                (residual_hbm, residual_in),
                (freq_hbm, freq_in),
                (variant_hbm, variant_in),
                (block_gene_hbm, block_gene_in),
                (counts_hbm, counts_in),
            )
        )
    ]
    for load in loads:
        load.start()

    def signal(semaphore, samp_to, gene_to):
        pl.semaphore_signal(
            semaphore,
            inc=1,
            device_id={"samp": samp_to, "gene": gene_to},
            device_id_type=MESH,
        )

    barrier = pltpu.get_barrier_semaphore()
    for gene_to in range(gene_size):

        @pl.when(gene_to > gene)
        def _(gene_to=gene_to):
            signal(barrier, samp, gene_to)

    @pl.loop(samp + 1, samp_size)
    def _(samp_to):
        for gene_to in range(gene_size):
            signal(barrier, samp_to, gene_to)

    loads[1].wait()
    loads[2].wait()
    own_weight, own_residual = weight_in[...], residual_in[...]
    own_tile = jnp.concatenate(
        [own_weight[:half], own_weight[half:], own_residual[:half], own_residual[half:]], axis=1
    )
    tile_out[...] = own_tile
    tiles[samp] = own_tile

    @pl.when(me > 0)
    def _():
        pl.semaphore_wait(barrier, me)

    @pl.loop(0, samp)
    def _(samp_to):
        signal(ready_sem.at[samp], samp_to, gene)

    loads[0].wait()

    def tile_copy(peer, slot):
        return pltpu.make_async_remote_copy(
            src_ref=tile_out,
            dst_ref=tiles.at[samp],
            send_sem=send_sem.at[0],
            recv_sem=tile_sem.at[slot],
            device_id={"samp": peer, "gene": gene},
            device_id_type=MESH,
        )

    def word_copy(peer, slot):
        start = pl.multiple_of(peer * (owned * BLK), BLK)
        return pltpu.make_async_remote_copy(
            src_ref=words_in.at[:, pl.ds(start, owned * BLK)],
            dst_ref=words.at[pl.ds(pl.multiple_of(samp * local_rows, local_rows), local_rows), :],
            send_sem=send_sem.at[1],
            recv_sem=word_sem.at[slot],
            device_id={"samp": peer, "gene": gene},
            device_id_type=MESH,
        )

    @pl.loop(0, samp)
    def _(peer):
        tile_copy(peer, samp).start()
        word_copy(peer, samp).start()

    for gene_to in range(gene_size):

        @pl.when(gene_to < gene)
        def _(gene_to=gene_to):
            signal(others_sem, samp, gene_to)

        @pl.when(gene_to != gene)
        def _(gene_to=gene_to):
            @pl.loop(0, samp)
            def _(samp_to):
                signal(others_sem, samp_to, gene_to)

    own_start = pl.multiple_of(samp * (owned * BLK), BLK)
    own_place = pl.multiple_of(samp * local_rows, local_rows)
    words[pl.ds(own_place, local_rows), :] = words_in[:, pl.ds(own_start, owned * BLK)]

    for load in loads[3:]:
        load.wait()
    block_gene = block_gene_in[...].astype(jnp.float32)
    counts = counts_in[...].astype(jnp.float32)
    block_lane = lax.broadcasted_iota(jnp.int32, block_gene.shape, 1)
    gene_lane = lax.broadcasted_iota(jnp.int32, counts.shape, 1).astype(jnp.float32)
    column = lax.broadcasted_iota(jnp.int32, (1, BLK), 1).astype(jnp.float32)
    stat_sub = lax.broadcasted_iota(jnp.int32, (8, width), 0)
    stat_lane = lax.broadcasted_iota(jnp.int32, (8, width), 1) - stat_sub * genes
    effective, places, twice = [], [], []
    for block in range(owned):
        local_block = samp * owned + block
        block_id = gene * local_blocks + local_block
        gene_of = lane_sum(jnp.where(block_lane == block_id, block_gene, 0.0))
        first = lane_sum(jnp.where(block_gene < gene_of, 1.0, 0.0))
        counted = lane_sum(jnp.where(gene_lane == gene_of, counts, 0.0))
        block_float = jnp.zeros((1, 1), jnp.float32) + block_id.astype(jnp.float32)
        live = (block_float - first) * BLK + column < counted
        weights = jnp.where(live, variant_in[pl.ds(local_block, 1), :], 0.0)
        effective.append(weights)
        across = jnp.broadcast_to(weights, (BLK, BLK))
        pair_weight[block] = across * across.T
        twice.append(2.0 * jnp.broadcast_to(freq_in[pl.ds(local_block, 1), :], (BLK, BLK)).T)
        member = stat_lane.astype(jnp.float32) == gene_of
        places.append(jnp.where(member & (stat_sub < STATS), 1.0, 0.0))

    def wait_tile(peer):
        pltpu.make_async_copy(tile_out, tiles.at[peer], tile_sem.at[peer]).wait()

    def wait_words(peer):
        place = words.at[pl.ds(pl.multiple_of(peer * local_rows, local_rows), local_rows), :]
        pltpu.make_async_copy(place, place, word_sem.at[peer]).wait()

    @pl.loop(samp + 1, samp_size)
    def _(peer):
        pl.semaphore_wait(ready_sem.at[peer], 1)
        tile_copy(peer, samp).start()
        word_copy(peer, samp).start()

    own_chunk = lax.div(samp, group)

    def add_chunk(step, totals):
        chunk = lax.rem(own_chunk + step, chunks)
        for place in range(group):

            @pl.when(chunk * group + place != samp)
            def _(peer=chunk * group + place):
                wait_tile(peer)

        parts = [tiles[chunk * group + place] for place in range(group)]
        kinds = [
            jnp.concatenate(
                [part[:, kind * local_rows : (kind + 1) * local_rows] for part in parts], axis=1
            )
            for kind in range(4)
        ]
        power = jnp.zeros((half, BLK), jnp.float32)
        for upper in range(2):
            weight, resid = kinds[upper], kinds[2 + upper]
            root = jnp.sqrt(weight)
            power = power + weight * resid * resid
            root_rows[upper * half : (upper + 1) * half, :] = root
            residual_rows[upper * half : (upper + 1) * half, :] = root * resid
        power_rows[chunk] = power
        for place in range(group):

            @pl.when(chunk * group + place != samp)
            def _(peer=chunk * group + place):
                wait_words(peer)

        start = pl.multiple_of(chunk * BLK, BLK)
        results = []
        for block in range(owned):
            turned = words[pl.ds(start, BLK), block * BLK : (block + 1) * BLK].T
            for field in range(fields):
                dosage = jnp.bitwise_and(jnp.right_shift(turned, 2 * field), 3)
                root = root_rows[field : field + 1, :]
                value = (root * (dosage.astype(jnp.float32) - twice[block])).astype(jnp.bfloat16)
                score = residual_rows[field : field + 1, :]
                lanes = slice(field * BLK, (field + 1) * BLK)
                scaled[:BLK, lanes] = value
                scaled[BLK:, lanes] = jnp.broadcast_to(score, (16, BLK)).astype(jnp.bfloat16)
            results.append(
                totals[block]
                + lax.dot_general(
                    scaled[...],
                    scaled[:BLK, :],
                    (((1,), (1,)), ((), ())),
                    preferred_element_type=jnp.float32,
                )
            )
        return tuple(results)

    totals = tuple(jnp.zeros((BLK + 16, BLK), jnp.float32) for _ in range(owned))
    if chunks <= 2:
        for step in range(chunks):
            totals = add_chunk(step, totals)
    else:
        totals = lax.fori_loop(0, chunks, add_chunk, totals)

    message = jnp.zeros((8, width), jnp.float32)
    diagonal = lax.broadcasted_iota(jnp.int32, (BLK, BLK), 0) == lax.broadcasted_iota(
        jnp.int32, (BLK, BLK), 1
    )
    for block in range(owned):
        total = totals[block]
        weighted = total[:BLK] * pair_weight[block]
        score = effective[block] * total[BLK : BLK + 1]
        sums = [
            score,
            jnp.sum(weighted, axis=0, keepdims=True),
            score * score,
            jnp.sum(jnp.where(diagonal, weighted, 0.0), axis=0, keepdims=True),
            jnp.sum(weighted * weighted, axis=0, keepdims=True),
            jnp.zeros((8 - STATS, BLK), jnp.float32),
        ]
        message = message + lane_sum(jnp.concatenate(sums, axis=0)) * places[block]
    row = jnp.sum(message, axis=0, keepdims=True)
    others = (samp_size - 1 - samp) * (gene_size - 1) + gene_size - 1 - gene

    @pl.when(others > 0)
    def _():
        pl.semaphore_wait(others_sem, others)

    row_out[...] = row
    rows[me] = row

    def row_copy(samp_to, gene_to):
        return pltpu.make_async_remote_copy(
            src_ref=row_out,
            dst_ref=rows.at[me],
            send_sem=row_send_sem,
            recv_sem=row_sem,
            device_id={"samp": samp_to, "gene": gene_to},
            device_id_type=MESH,
        )

    @pl.loop(1, samp_size)
    def _(step):
        samp_to = samp + step
        samp_to = jnp.where(samp_to >= samp_size, samp_to - samp_size, samp_to)
        for gene_to in range(gene_size):
            row_copy(samp_to, gene_to).start()

    for gene_to in range(gene_size):

        @pl.when(gene_to != gene)
        def _(gene_to=gene_to):
            row_copy(samp, gene_to).start()

    power = jnp.sum(power_rows[...], axis=0)
    variance = lane_sum(jnp.sum(power, axis=0, keepdims=True)) / (
        fields * local_rows * samp_size
    )
    landed = rows.at[pl.ds(0, devices - 1)]
    pltpu.make_async_copy(landed, landed, row_sem).wait()
    totals = jnp.sum(rows[...], axis=0)
    parts = [totals[:, stat * genes : (stat + 1) * genes] for stat in range(STATS)]
    both_ref[0:1] = parts[0] / jnp.sqrt(variance * parts[1])
    both_ref[1:2] = (parts[2] - variance * parts[3]) / (
        variance * jnp.sqrt(2.0 * parts[4])
    )

    pltpu.make_async_copy(landed, landed, row_send_sem).wait()

    sent_tiles = tiles.at[pl.ds(0, samp_size - 1)]
    pltpu.make_async_copy(sent_tiles, sent_tiles, send_sem.at[0]).wait()
    sent_words = words.at[pl.ds(0, (samp_size - 1) * local_rows), :]
    pltpu.make_async_copy(sent_words, sent_words, send_sem.at[1]).wait()


def solution(mesh):
    samp_size, gene_size = mesh.shape["samp"], mesh.shape["gene"]
    devices = samp_size * gene_size

    def local(
        genotypes, allele_freq, sample_weight, residual, variant_weight, block_gene, gene_variants
    ):
        local_rows, columns = genotypes.shape
        local_blocks = columns // BLK
        owned = local_blocks // samp_size
        fields = sample_weight.shape[0]
        genes = gene_variants.shape[0]
        width = -(-STATS * genes // BLK) * BLK
        chunks = samp_size * local_rows // BLK
        both = pl.pallas_call(
            functools.partial(kernel, samp_size, gene_size),
            out_shape=pltpu.VMEM((2, genes), jnp.float32),
            in_specs=[pl.BlockSpec(memory_space=pl.ANY)] * 7,
            out_specs=pl.BlockSpec(memory_space=pltpu.VMEM),
            scratch_shapes=[
                pltpu.VMEM((local_rows, columns), jnp.int32),
                pltpu.VMEM((local_blocks, BLK), jnp.float32),
                pltpu.VMEM((fields, local_rows), jnp.float32),
                pltpu.VMEM((fields, local_rows), jnp.float32),
                pltpu.VMEM((local_blocks, BLK), jnp.float32),
                pltpu.VMEM((1, block_gene.shape[0]), jnp.int32),
                pltpu.VMEM((1, genes), jnp.int32),
                pltpu.VMEM((fields // 2, 4 * local_rows), jnp.float32),
                pltpu.VMEM((samp_size, fields // 2, 4 * local_rows), jnp.float32),
                pltpu.VMEM((samp_size * local_rows, owned * BLK), jnp.int32),
                pltpu.VMEM((BLK + 16, fields * BLK), jnp.bfloat16),
                pltpu.VMEM((fields, BLK), jnp.float32),
                pltpu.VMEM((fields, BLK), jnp.float32),
                pltpu.VMEM((chunks, fields // 2, BLK), jnp.float32),
                pltpu.VMEM((owned, BLK, BLK), jnp.float32),
                pltpu.VMEM((1, width), jnp.float32),
                pltpu.VMEM((devices, 1, width), jnp.float32),
                pltpu.SemaphoreType.DMA((7,)),
                pltpu.SemaphoreType.DMA((2,)),
                pltpu.SemaphoreType.DMA((samp_size,)),
                pltpu.SemaphoreType.DMA((samp_size,)),
                pltpu.SemaphoreType.DMA,
                pltpu.SemaphoreType.DMA,
                pltpu.SemaphoreType.REGULAR((samp_size,)),
                pltpu.SemaphoreType.REGULAR,
            ],
            compiler_params=pltpu.CompilerParams(collective_id=0, has_side_effects=True),
        )(
            genotypes,
            allele_freq.reshape(local_blocks, BLK),
            sample_weight,
            residual,
            variant_weight.reshape(local_blocks, BLK),
            block_gene.reshape(1, -1),
            gene_variants.reshape(1, -1),
        )
        return both[0], both[1]

    placed = (P("samp", "gene"), P("gene"), P(None, "samp"), P(None, "samp"), P("gene"), P(), P())
    return jax.shard_map(local, mesh=mesh, in_specs=placed, out_specs=(P(), P()), check_vma=False)
```

time: 21.7 us -> 19 us (0.88)
  Pallas kernels: 19 us -> 17.7 us
  local copies, waits for them, and re-layouts: 1.8 us -> 0.52 us
    unnamed x6 -> x0, local copies, waits for them, and re-layouts: 1.8 us -> none
    pallas_call x1, Pallas kernels: 19 us -> 17.7 us  [local(): pl.pallas_call(functools.partial(kernel, samp_size, gene_size), out_shape...]
    squeeze x0 -> x1, local copies, waits for them, and re-layouts: none -> 0.52 us  [local(): return (both[0], both[1])]
where the time goes in v2:
time: 19 us; the launch traced here: 18.9 us
  Pallas kernels  17.7 us (93%)
  between operations  0.64 us (3%)
  local copies, waits for them, and re-layouts  0.52 us (3%)
    pallas_call x1, Pallas kernels, local(): pl.pallas_call(functools.partial(kernel, samp_size, gene_size), out_shape...  17.7 us
    squeeze x1, local copies, waits for them, and re-layouts, local(): return (both[0], both[1])  0.52 us

profile of v2, /device:TPU:0, one launch (start us, length us, event | category | flops | bytes accessed | tf_op | source)
XLA Modules:
  0.0 18.9 jit_solution(8639446678878444653)
XLA Ops:
  0.6 17.7 %shard_map.86 = f32[2,16]{1,0:T(2,128)S(1)} custom-call(s32[32,1024]{1,0:T(8,128)} %genotypes_hbm.1, f32[8,128]{1,0:T(8,128)} %bitcast.8, f32[16,32]{1,0:T(8,128)} %weight_hbm.1, f32[16,32]{1,0:T(8,128)} %residual_hbm.1, f32[8,128]{1,0:T(8,128)} %bitcast.9, s32[1,32]{1,0:T(1,128)} %bitcast.10, s32[1,16]{1,0:T(1,128)} %bitcast.11), custom_call_target="tpu_custom_call" | custom-call | tf_op jit(solution)/shard_map/pallas_call | solution.py:352
  18.3 0.5 %slice_bitcast_fusion = (f32[16]{0:T(128)}, f32[16]{0:T(128)}) fusion(f32[2,16]{1,0:T(2,128)S(1)} %shard_map.86), kind=kLoop, calls=%fused_computation | loop fusion | bytes 256 | tf_op jit(solution)/shard_map/squeeze | solution.py:394

commit v3 on v2

--- a/solution.py
+++ b/solution.py
@@ -37,6 +37,7 @@
     tile_out,
     tiles,
     words,
+    relay,
     scaled,
     root_rows,
     residual_rows,
@@ -45,9 +46,11 @@
     row_out,
     rows,
     load_sem,
-    send_sem,
+    tile_send_sem,
+    word_send_sem,
     tile_sem,
     word_sem,
+    relay_sem,
     row_send_sem,
     row_sem,
     ready_sem,
@@ -122,31 +125,69 @@
 
     loads[0].wait()
 
-    def tile_copy(peer, slot):
+    inner = 2 if samp_size % 2 == 0 else 1
+    plane = lax.div(samp, inner)
+    behind = samp - inner
+    far_start = jnp.minimum((plane + 3) * inner, samp_size)
+    forward_start = jnp.where(plane > 0, jnp.minimum((plane + 2) * inner, samp_size), samp_size)
+
+    def place_of(peer):
+        return words.at[pl.ds(pl.multiple_of(peer * local_rows, local_rows), local_rows), :]
+
+    def columns_of(peer):
+        return words_in.at[:, pl.ds(pl.multiple_of(peer * (owned * BLK), BLK), owned * BLK)]
+
+    def remote(source, target, send, receive, peer):
         return pltpu.make_async_remote_copy(
-            src_ref=tile_out,
-            dst_ref=tiles.at[samp],
-            send_sem=send_sem.at[0],
-            recv_sem=tile_sem.at[slot],
+            src_ref=source,
+            dst_ref=target,
+            send_sem=send,
+            recv_sem=receive,
             device_id={"samp": peer, "gene": gene},
             device_id_type=MESH,
         )
 
-    def word_copy(peer, slot):
-        start = pl.multiple_of(peer * (owned * BLK), BLK)
-        return pltpu.make_async_remote_copy(
-            src_ref=words_in.at[:, pl.ds(start, owned * BLK)],
-            dst_ref=words.at[pl.ds(pl.multiple_of(samp * local_rows, local_rows), local_rows), :],
-            send_sem=send_sem.at[1],
-            recv_sem=word_sem.at[slot],
-            device_id={"samp": peer, "gene": gene},
-            device_id_type=MESH,
+    def tile_copy(peer):
+        return remote(
+            tile_out, tiles.at[samp], tile_send_sem.at[peer], tile_sem.at[samp], peer
+        )
+
+    def word_copy(peer):
+        return remote(
+            columns_of(peer), place_of(samp), word_send_sem.at[peer], word_sem.at[samp], peer
+        )
+
+    def relay_copy(peer):
+        return remote(
+            columns_of(peer),
+            relay.at[peer],
+            word_send_sem.at[peer],
+            relay_sem.at[peer],
+            samp + inner,
+        )
+
+    def forward_tile(peer):
+        return remote(
+            tiles.at[behind],
+            tiles.at[behind],
+            tile_send_sem.at[samp_size + peer],
+            tile_sem.at[behind],
+            peer,
+        )
+
+    def forward_words(peer):
+        return remote(
+            relay.at[peer],
+            place_of(behind),
+            word_send_sem.at[samp_size + peer],
+            word_sem.at[behind],
+            peer,
         )
 
     @pl.loop(0, samp)
     def _(peer):
-        tile_copy(peer, samp).start()
-        word_copy(peer, samp).start()
+        tile_copy(peer).start()
+        word_copy(peer).start()
 
     for gene_to in range(gene_size):
 
@@ -194,14 +235,40 @@
         pltpu.make_async_copy(tile_out, tiles.at[peer], tile_sem.at[peer]).wait()
 
     def wait_words(peer):
-        place = words.at[pl.ds(pl.multiple_of(peer * local_rows, local_rows), local_rows), :]
+        place = place_of(peer)
         pltpu.make_async_copy(place, place, word_sem.at[peer]).wait()
 
-    @pl.loop(samp + 1, samp_size)
+    @pl.when(plane > 0)
+    def _():
+        wait_tile(behind)
+
+    @pl.loop(samp + 1, far_start)
     def _(peer):
         pl.semaphore_wait(ready_sem.at[peer], 1)
-        tile_copy(peer, samp).start()
-        word_copy(peer, samp).start()
+
+        @pl.when(peer >= forward_start)
+        def _():
+            forward_tile(peer).start()
+            pltpu.make_async_copy(relay.at[peer], relay.at[peer], relay_sem.at[peer]).wait()
+            forward_words(peer).start()
+
+        tile_copy(peer).start()
+        word_copy(peer).start()
+
+        @pl.when(peer == samp + inner)
+        def _():
+            @pl.loop(far_start, samp_size)
+            def _(far):
+                relay_copy(far).start()
+
+    @pl.loop(far_start, samp_size)
+    def _(peer):
+        @pl.when(peer >= forward_start)
+        def _():
+            pl.semaphore_wait(ready_sem.at[peer], 1)
+            forward_tile(peer).start()
+            pltpu.make_async_copy(relay.at[peer], relay.at[peer], relay_sem.at[peer]).wait()
+            forward_words(peer).start()
 
     own_chunk = lax.div(samp, group)
 
@@ -209,7 +276,7 @@
         chunk = lax.rem(own_chunk + step, chunks)
         for place in range(group):
 
-            @pl.when(chunk * group + place != samp)
+            @pl.when((chunk * group + place != samp) & (chunk * group + place != behind))
             def _(peer=chunk * group + place):
                 wait_tile(peer)
 
@@ -282,6 +349,12 @@
         ]
         message = message + lane_sum(jnp.concatenate(sums, axis=0)) * places[block]
     row = jnp.sum(message, axis=0, keepdims=True)
+    @pl.loop(far_start, samp_size)
+    def _(peer):
+        @pl.when(plane == 0)
+        def _():
+            pl.semaphore_wait(ready_sem.at[peer], 1)
+
     others = (samp_size - 1 - samp) * (gene_size - 1) + gene_size - 1 - gene
 
     @pl.when(others > 0)
@@ -303,10 +376,17 @@
 
     @pl.loop(1, samp_size)
     def _(step):
-        samp_to = samp + step
-        samp_to = jnp.where(samp_to >= samp_size, samp_to - samp_size, samp_to)
-        for gene_to in range(gene_size):
-            row_copy(samp_to, gene_to).start()
+        gap = samp_size - step
+
+        @pl.when(samp + gap < samp_size)
+        def _():
+            for gene_to in range(gene_size):
+                row_copy(samp + gap, gene_to).start()
+
+        @pl.when(samp - gap >= 0)
+        def _():
+            for gene_to in range(gene_size):
+                row_copy(samp - gap, gene_to).start()
 
     for gene_to in range(gene_size):
 
@@ -329,10 +409,20 @@
 
     pltpu.make_async_copy(landed, landed, row_send_sem).wait()
 
-    sent_tiles = tiles.at[pl.ds(0, samp_size - 1)]
-    pltpu.make_async_copy(sent_tiles, sent_tiles, send_sem.at[0]).wait()
-    sent_words = words.at[pl.ds(0, (samp_size - 1) * local_rows), :]
-    pltpu.make_async_copy(sent_words, sent_words, send_sem.at[1]).wait()
+    @pl.loop(0, samp_size)
+    def _(peer):
+        @pl.when((peer != samp) & (peer < far_start))
+        def _():
+            tile_copy(peer).wait_send()
+
+        @pl.when(peer != samp)
+        def _():
+            word_copy(peer).wait_send()
+
+        @pl.when(peer >= forward_start)
+        def _():
+            forward_tile(peer).wait_send()
+            forward_words(peer).wait_send()
 
 
 def solution(mesh):
@@ -365,6 +455,7 @@
                 pltpu.VMEM((fields // 2, 4 * local_rows), jnp.float32),
                 pltpu.VMEM((samp_size, fields // 2, 4 * local_rows), jnp.float32),
                 pltpu.VMEM((samp_size * local_rows, owned * BLK), jnp.int32),
+                pltpu.VMEM((samp_size, local_rows, owned * BLK), jnp.int32),
                 pltpu.VMEM((BLK + 16, fields * BLK), jnp.bfloat16),
                 pltpu.VMEM((fields, BLK), jnp.float32),
                 pltpu.VMEM((fields, BLK), jnp.float32),
@@ -373,7 +464,9 @@
                 pltpu.VMEM((1, width), jnp.float32),
                 pltpu.VMEM((devices, 1, width), jnp.float32),
                 pltpu.SemaphoreType.DMA((7,)),
-                pltpu.SemaphoreType.DMA((2,)),
+                pltpu.SemaphoreType.DMA((2 * samp_size,)),
+                pltpu.SemaphoreType.DMA((2 * samp_size,)),
+                pltpu.SemaphoreType.DMA((samp_size,)),
                 pltpu.SemaphoreType.DMA((samp_size,)),
                 pltpu.SemaphoreType.DMA((samp_size,)),
                 pltpu.SemaphoreType.DMA,

time: 19 us -> 23.3 us (1.23)
  Pallas kernels: 17.7 us -> 22 us
    pallas_call x1, Pallas kernels: 17.7 us -> 22 us  [local(): pl.pallas_call(functools.partial(kernel, samp_size, gene_size), out_shape...]
where the time goes in v3:
time: 23.3 us; the launch traced here: 23.2 us
  Pallas kernels  22 us (94%)
  between operations  0.64 us (3%)
  local copies, waits for them, and re-layouts  0.52 us (2%)
    pallas_call x1, Pallas kernels, local(): pl.pallas_call(functools.partial(kernel, samp_size, gene_size), out_shape...  22 us
    squeeze x1, local copies, waits for them, and re-layouts, local(): return (both[0], both[1])  0.52 us

profile of v3, /device:TPU:0, one launch (start us, length us, event | category | flops | bytes accessed | tf_op | source)
XLA Modules:
  0.0 23.2 jit_solution(8614005010896706164)
XLA Ops:
  0.6 22.0 %shard_map.86 = f32[2,16]{1,0:T(2,128)S(1)} custom-call(s32[32,1024]{1,0:T(8,128)} %genotypes_hbm.1, f32[8,128]{1,0:T(8,128)} %bitcast.8, f32[16,32]{1,0:T(8,128)} %weight_hbm.1, f32[16,32]{1,0:T(8,128)} %residual_hbm.1, f32[8,128]{1,0:T(8,128)} %bitcast.9, s32[1,32]{1,0:T(1,128)} %bitcast.10, s32[1,16]{1,0:T(1,128)} %bitcast.11), custom_call_target="tpu_custom_call" | custom-call | tf_op jit(solution)/shard_map/pallas_call | solution.py:442
  22.7 0.5 %slice_bitcast_fusion = (f32[16]{0:T(128)}, f32[16]{0:T(128)}) fusion(f32[2,16]{1,0:T(2,128)S(1)} %shard_map.86), kind=kLoop, calls=%fused_computation | loop fusion | bytes 256 | tf_op jit(solution)/shard_map/squeeze | solution.py:487

commit v4 on v2

--- a/solution.py
+++ b/solution.py
@@ -120,8 +120,6 @@
     def _(samp_to):
         signal(ready_sem.at[samp], samp_to, gene)
 
-    loads[0].wait()
-
     def tile_copy(peer, slot):
         return pltpu.make_async_remote_copy(
             src_ref=tile_out,
@@ -146,6 +144,11 @@
     @pl.loop(0, samp)
     def _(peer):
         tile_copy(peer, samp).start()
+
+    loads[0].wait()
+
+    @pl.loop(0, samp)
+    def _(peer):
         word_copy(peer, samp).start()
 
     for gene_to in range(gene_size):
@@ -303,10 +306,17 @@
 
     @pl.loop(1, samp_size)
     def _(step):
-        samp_to = samp + step
-        samp_to = jnp.where(samp_to >= samp_size, samp_to - samp_size, samp_to)
-        for gene_to in range(gene_size):
-            row_copy(samp_to, gene_to).start()
+        gap = samp_size - step
+
+        @pl.when(samp + gap < samp_size)
+        def _():
+            for gene_to in range(gene_size):
+                row_copy(samp + gap, gene_to).start()
+
+        @pl.when(samp - gap >= 0)
+        def _():
+            for gene_to in range(gene_size):
+                row_copy(samp - gap, gene_to).start()
 
     for gene_to in range(gene_size):
 

time: 19 us -> 18.9 us (level)
  no operation moved by 1% of the time
where the time goes in v4:
time: 18.9 us; the launch traced here: 18.8 us
  Pallas kernels  17.6 us (93%)
  between operations  0.64 us (3%)
  local copies, waits for them, and re-layouts  0.52 us (3%)
    pallas_call x1, Pallas kernels, local(): pl.pallas_call(functools.partial(kernel, samp_size, gene_size), out_shape...  17.6 us
    squeeze x1, local copies, waits for them, and re-layouts, local(): return (both[0], both[1])  0.52 us

profile of v4, /device:TPU:0, one launch (start us, length us, event | category | flops | bytes accessed | tf_op | source)
XLA Modules:
  0.0 18.8 jit_solution(2864466939183314457)
XLA Ops:
  0.6 17.6 %shard_map.86 = f32[2,16]{1,0:T(2,128)S(1)} custom-call(s32[32,1024]{1,0:T(8,128)} %genotypes_hbm.1, f32[8,128]{1,0:T(8,128)} %bitcast.8, f32[16,32]{1,0:T(8,128)} %weight_hbm.1, f32[16,32]{1,0:T(8,128)} %residual_hbm.1, f32[8,128]{1,0:T(8,128)} %bitcast.9, s32[1,32]{1,0:T(1,128)} %bitcast.10, s32[1,16]{1,0:T(1,128)} %bitcast.11), custom_call_target="tpu_custom_call" | custom-call | tf_op jit(solution)/shard_map/pallas_call | solution.py:362
  18.3 0.5 %slice_bitcast_fusion = (f32[16]{0:T(128)}, f32[16]{0:T(128)}) fusion(f32[2,16]{1,0:T(2,128)S(1)} %shard_map.86), kind=kLoop, calls=%fused_computation | loop fusion | bytes 256 | tf_op jit(solution)/shard_map/squeeze | solution.py:404
